TPU v7x, 512 devices: a whole 4x8x8 slice. The times are simulated.
512 devices in a mesh: pipe: 16 (over y, core), tensor: 32 (over z, x).
Axes of the slice: x: 4, y: 8, z: 8, core: 2. Of those that a mesh axis runs over, the one named last changes fastest.
Arguments:
- patches: bfloat16 [262144, 1280], P(('pipe', 'tensor')), may hold values from -6 to 6
- attn_gain: float32 [1280], replicated, may hold values from 0.25 to 1.75
- w_qkv: bfloat16 [1280, 3840], P('tensor', 'pipe'), may hold values from -0.1118034 to 0.1118034
- w_out: bfloat16 [1280, 1280], P('tensor', 'pipe'), may hold values from -0.15625 to 0.15625
- merge_gain: float32 [1280], replicated, may hold values from 0.25 to 1.75
- window_ids: int32 [262144], P(('pipe', 'tensor')), may hold values from 0 to 127, as said below
- image_patches: int32 [2048], P(('pipe', 'tensor')), may hold values from 0 to 512, as said below
- image_sample: int32 [2048], P(('pipe', 'tensor')), may hold values from 0 to 7
Outputs:
- vision_seq: bfloat16 [16, 128, 32, 5120], P('pipe', None, 'tensor')
Inputs may be any that keep to these rules, and one draw needn't show every extreme that they name: `window_ids`: Non-decreasing within each bundle and equal over each 4 consecutive slots; every window lies within one aligned block of 64 slots of a bundle. `image_patches`: multiples of 128; the images of one bundle take at most 512 slots and at least half of them, and in every micro-batch some bundle is full.
All inputs are finite; a program needn't handle non-finite values.
Results may differ from a plain program's by a relative error of at most 0.0053.
Values may be sent and summed in bfloat16 or wider, within the bound.
No kernel may reach another device: no remote copies, remote signals or barrier semaphores. Data moves between devices by JAX's collectives and lax.ppermute only.
A program may use at most 64 MiB of HBM per device.

v0:
```python
import math
import jax
import jax.numpy as jnp
from jax import lax
from jax.sharding import PartitionSpec as P

HEADS = 16
WINDOW = 64
SAMPLES = 8
epsilon = 1e-06


def joined_along(blocks, dim):
    dims = list(blocks.shape[1:])
    dims[dim] *= blocks.shape[0]
    return jnp.moveaxis(blocks, 0, dim).reshape(dims)


def copy_for_each(x, axis):
    size = lax.axis_size(axis)
    return lax.all_to_all(jnp.broadcast_to(x[None], (size, *x.shape)), axis, 0, 0, tiled=True)


def gather_directly(x, axis, dim):
    return joined_along(copy_for_each(x, axis), dim)


def normalize(values, gain_row):
    return (
        values * lax.rsqrt(jnp.mean(values * values, axis=-1, keepdims=True) + epsilon) * gain_row
    )


def token_positions(starts, merged_count, token_count):
    offsets = jnp.cumsum(merged_count) - merged_count
    token_index = jnp.arange(token_count, dtype=jnp.int32)
    inside = (token_index[None, :] >= offsets[:, None]) & (
        token_index[None, :] < (offsets + merged_count)[:, None]
    )
    position = jnp.sum(
        jnp.where(inside, starts[:, None] + token_index[None, :] - offsets[:, None], 0), axis=0
    )
    return jnp.where(jnp.any(inside, axis=0), position, -1)


def body(patches, attn_gain, w_qkv, w_out, merge_gain, window_ids, image_patches, image_sample):
    patch_count, feature_width = patches.shape
    token_count = patch_count // 4
    group_size = lax.axis_size("tensor")
    own_index = lax.axis_index("tensor")
    residual = patches.astype(jnp.float32)
    normed = normalize(residual, attn_gain).astype(jnp.bfloat16)
    qkv_rows = gather_directly(w_qkv, "tensor", 0)
    qkv = jnp.dot(
        normed,
        lax.all_gather(qkv_rows, "pipe", axis=1, tiled=True),
        preferred_element_type=jnp.float32,
    ).astype(jnp.bfloat16)
    head_width = feature_width // HEADS
    tile_count = patch_count // WINDOW

    def split_heads(block):
        return block.reshape(tile_count, WINDOW, HEADS, head_width)

    queries = split_heads(qkv[:, :feature_width])
    keys_tile = split_heads(qkv[:, feature_width : 2 * feature_width])
    values_tile = split_heads(qkv[:, 2 * feature_width :])
    scores = jnp.einsum(
        "tqhd,tkhd->thqk", queries, keys_tile, preferred_element_type=jnp.float32
    ) * (1.0 / math.sqrt(head_width))
    live_row = jnp.arange(patch_count, dtype=jnp.int32) < jnp.sum(image_patches)
    window_tile = window_ids.reshape(tile_count, WINDOW)
    live_tile = live_row.reshape(tile_count, WINDOW)
    allowed = (window_tile[:, :, None] == window_tile[:, None, :]) & live_tile[:, None, :]
    scores = jnp.where(allowed[:, None, :, :], scores, -1e30)
    row_max = jnp.max(scores, axis=-1, keepdims=True)
    exponent = jnp.exp(scores - row_max)
    weights = (exponent / jnp.sum(exponent, axis=-1, keepdims=True)).astype(jnp.bfloat16)
    context = jnp.einsum(
        "thqk,tkhd->tqhd", weights, values_tile, preferred_element_type=jnp.float32
    ).reshape(patch_count, feature_width)
    context = jnp.where(live_row[:, None], context, 0.0).astype(jnp.bfloat16)
    proj_rows = lax.all_gather(w_out, "tensor", axis=0, tiled=True)
    attended = jnp.dot(
        context,
        lax.all_gather(proj_rows, "pipe", axis=1, tiled=True),
        preferred_element_type=jnp.float32,
    )
    hidden = residual + attended
    merged = (
        normalize(hidden, merge_gain).astype(jnp.bfloat16).reshape(token_count, 4 * feature_width)
    )
    outgoing = merged.reshape(token_count // group_size, group_size, 4 * feature_width)
    merged_count = image_patches // 4
    sample_hot = image_sample[:, None] == jnp.arange(SAMPLES, dtype=jnp.int32)[None, :]
    sample_tally = jnp.sum(jnp.where(sample_hot, merged_count[:, None], 0), axis=0)
    all_tallies = gather_directly(sample_tally[None, :], "tensor", 0)
    source_ranks = jnp.arange(group_size, dtype=jnp.int32)
    before = jnp.sum(jnp.where((source_ranks < own_index)[:, None], all_tallies, 0), axis=0)
    totals = jnp.sum(all_tallies, axis=0)
    sample_index = jnp.arange(SAMPLES, dtype=jnp.int32)
    sample_base = jnp.sum(
        jnp.where(sample_index[None, :] < sample_index[:, None], totals[None, :], 0), axis=1
    )
    image_order = jnp.arange(image_sample.shape[0], dtype=jnp.int32)
    same_before = (image_sample[None, :] == image_sample[:, None]) & (
        image_order[None, :] < image_order[:, None]
    )
    earlier = jnp.sum(jnp.where(same_before, merged_count[None, :], 0), axis=1)
    starts = jnp.sum(jnp.where(sample_hot, (sample_base + before)[None, :], 0), axis=1) + earlier
    position = token_positions(starts, merged_count, token_count)
    outgoing_position = position.reshape(token_count // group_size, group_size)
    received, received_position = (
        lax.all_to_all(outgoing, "tensor", split_axis=1, concat_axis=0, tiled=True),
        lax.all_to_all(outgoing_position, "tensor", split_axis=1, concat_axis=0, tiled=True),
    )
    dest_rows = received_position.reshape(token_count) // group_size
    placement = (jnp.arange(token_count, dtype=jnp.int32)[:, None] == dest_rows[None, :]).astype(
        jnp.bfloat16
    )
    placed = jnp.dot(
        placement,
        received.reshape(token_count, 4 * feature_width),
        preferred_element_type=jnp.float32,
    )
    return placed.astype(jnp.bfloat16).reshape(1, token_count, 1, 4 * feature_width)


def solution(mesh):
    return jax.shard_map(
        body,
        mesh=mesh,
        in_specs=(
            P(("pipe", "tensor"), None),
            P(),
            P("tensor", "pipe"),
            P("tensor", "pipe"),
            P(),
            P(("pipe", "tensor")),
            P(("pipe", "tensor")),
            P(("pipe", "tensor")),
        ),
        out_specs=P("pipe", None, "tensor", None),
        check_vma=False,
    )
```

profile of v0, /device:TPU:4, one launch (start us, length us, event | category | flops | bytes accessed | tf_op | source)
XLA Modules:
  0.0 208.7 jit_solution(4896109178755569658)
XLA Ops:
  6.5 0.0 copy-start.3
  6.6 0.0 all-gather.3.cloned.1.call-start
  6.6 0.9 broadcast_in_dim.144
  7.5 0.0 copy-start.7
  7.5 32.9 %all_to_all.38 = bf16[32,40,240]{2,1,0:T(8,128)(2,1)S(1)} all-to-all(bf16[32,40,240]{2,1,0:T(8,128)(2,1)S(1)} %broadcast_in_dim.144), channel_id=1, replica_groups=mesh['pipe'=16,'tensor'=32] {'tensor'}, dimensions={0} | all-to-all | bytes 1228800 | tf_op jit(solution)/shard_map/all_to_all | solution.py:21
  40.4 1.1 copy.60
  41.4 0.0 all-gather.3.cloned.1.call-update
  41.4 0.0 all-gather.5.cloned.1.call-start
  41.5 0.0 copy-done.3
  41.5 47.5 %all_gather.10 = bf16[1280,80]{1,0:T(8,128)(2,1)S(1)} all-gather(bf16[40,80]{1,0:T(8,128)(2,1)S(1)} %copy-done.3), channel_id=1, replica_groups=mesh['pipe'=16,'tensor'=32] {'tensor'}, dimensions={0}, use_global_device_ids=true | all-gather | bytes 211200 | tf_op jit(solution)/shard_map/all_gather | solution.py:83
  89.0 0.9 copy.66
  89.9 0.0 all-gather.5.cloned.1.call-update
  89.9 0.0 copy-done.8
  89.9 0.7 and_select_fusion.1
  90.6 0.0 copy-done.6
  90.6 0.1 select_reduce_fusion.5
  90.7 0.6 broadcast_in_dim.96
  91.3 6.7 %all-to-all-start = ((s32[32,1,8]{2,1,0:T(1,128)}), s32[32,1,8]{2,1,0:T(1,128)S(1)}, u32[]{:S(2)}, u32[]{:S(2)}) async-start(s32[32,1,8]{2,1,0:T(1,128)} %broadcast_in_dim.96), calls=%async_computation | async-start | bytes 32768 | tf_op jit(solution)/shard_map/all_to_all | solution.py:21
  98.0 0.0 copy-done.5
  98.0 0.1 eq.67
  98.1 0.2 reduce-window.8
  98.3 0.6 iota_compare_fusion.3
  98.9 0.6 add_compare_fusion
  99.6 0.2 select_reduce_fusion.3
  99.7 0.1 fusion.25
  99.8 0.0 copy-done.1
  99.8 0.3 fusion.3
  100.2 0.2 compare_and_fusion
  100.4 5.4 %all-to-all-done = s32[32,1,8]{2,1,0:T(1,128)S(1)} async-done(((s32[32,1,8]{2,1,0:T(1,128)}), s32[32,1,8]{2,1,0:T(1,128)S(1)}, u32[]{:S(2)}, u32[]{:S(2)}) %all-to-all-start) | async-done | bytes 1056 | tf_op jit(solution)/shard_map/all_to_all | solution.py:21
  105.8 0.1 reduce_sum.100
  105.8 0.1 select_reduce_fusion.1
  105.9 0.1 select_reduce_fusion
  106.0 0.2 select_reduce_fusion.4
  106.2 0.1 select_reduce_fusion.2
  106.3 0.1 select_n.69
  106.4 0.7 copy.59
  107.1 5.7 %all-to-all-start.1 = ((s32[4,32,1]{0,2,1:T(1,128)}), s32[4,32,1]{0,2,1:T(1,128)S(1)}, u32[]{:S(2)}, u32[]{:S(2)}) async-start(s32[4,32,1]{0,2,1:T(1,128)} %copy.59), calls=%async_computation.1 | async-start | bytes 32768 | tf_op jit(solution)/shard_map/all_to_all | solution.py:115
  112.8 0.0 all-gather.3.cloned.1.call-done
  112.9 0.0 copy-done.7
  112.9 9.5 %convolution_convert_fusion.1 = bf16[512,3840]{1,0:T(8,128)(2,1)S(1)} fusion(bf16[1280,3840]{0,1:T(8,128)(2,1)} %all-gather.3.cloned.1.call-done, bf16[512,1280]{1,0:T(8,128)(2,1)S(1)} %copy-done.1, f32[1280]{0:T(1024)S(1)} %copy-done.7, f32[512]{0:T(512)S(1)} %add_rsqrt_fusion.1), kind=kOutput, calls=%fused_computation.2 | convolution fusion | flops 5037752320 | bytes 15080448 | tf_op jit(solution)/shard_map/dot_general | solution.py:54
  122.4 1.7 fusion.26
  124.1 4.1 %reshape.170 = bf16[8,64,16,80]{3,2,1,0:T(8,128)(2,1)S(1)} reshape(bf16[512,1280]{1,0:T(8,128)(2,1)} %get-tuple-element.7) | data formatting | bytes 2621440 | tf_op jit(solution)/shard_map/reshape | solution.py:63
  128.2 5.1 %reshape.171 = bf16[8,64,16,80]{3,2,1,0:T(8,128)(2,1)} reshape(bf16[512,1280]{1,0:T(8,128)(2,1)} %get-tuple-element.6) | data formatting | bytes 2621440 | tf_op jit(solution)/shard_map/reshape | solution.py:63
  133.3 4.1 %reshape.169 = bf16[8,64,16,80]{3,2,1,0:T(8,128)(2,1)} reshape(bf16[512,1280]{1,0:T(8,128)(2,1)S(1)} %get-tuple-element.5) | data formatting | bytes 2621440 | tf_op jit(solution)/shard_map/reshape | solution.py:63
  137.4 2.8 %fusion.7 = f32[8,16,64,64]{2,3,1,0:T(8,128)S(1)} fusion(bf16[8,64,16,80]{3,2,1,0:T(8,128)(2,1)} %reshape.171, bf16[8,64,16,80]{3,2,1,0:T(8,128)(2,1)S(1)} %reshape.170), kind=kOutput, calls=%fused_computation.19 | convolution fusion | flops 83886080 | bytes 4718592 | tf_op jit(solution)/shard_map/tqhd,tkhd->thqk/dot_general | solution.py:68
  140.2 1.5 fusion.27
  141.7 0.1 copy-done
  141.8 1.2 convolution_bitcast_fusion
  143.0 1.4 copy.65
  144.4 0.0 copy-start.2
  144.4 3.3 %reshape.172 = bf16[512,1280]{1,0:T(8,128)(2,1)} reshape(bf16[8,64,16,80]{3,2,1,0:T(8,128)(2,1)S(1)} %copy.65) | data formatting | bytes 2621440 | tf_op jit(solution)/shard_map/reshape | solution.py:81
  147.6 0.2 all-gather.5.cloned.1.call-done
  147.8 0.0 copy-done.2
  147.8 4.4 %multiply_reduce_fusion = (f32[512]{0:T(512)S(1)}, f32[512,1280]{1,0:T(8,128)S(1)}) fusion(bf16[1280,1280]{0,1:T(8,128)(2,1)} %all-gather.5.cloned.1.call-done, bf16[512,1280]{1,0:T(8,128)(2,1)} %reshape.172, pred[512]{0:T(512)(128)(4,1)S(1)} %iota_compare_fusion.3, bf16[512,1280]{1,0:T(8,128)(2,1)S(1)} %copy-done.2), kind=kOutput, calls=%fused_computation.15 | convolution fusion | flops 1680997888 | bytes 8522240 | tf_op jit(solution)/shard_map/dot_general | solution.py:84
  152.2 0.0 copy-done.4
  152.2 0.3 multiply_convert_fusion
  152.5 0.8 reshape_reshape.3
  153.3 2.1 copy.67
  155.4 0.0 all-to-all-done.1
  155.4 10.5 %all-to-all-start.3 = ((bf16[4,32,5120]{2,0,1:T(4,128)(2,1)}), bf16[4,32,5120]{2,0,1:T(4,128)(2,1)S(1)}, u32[]{:S(2)}, u32[]{:S(2)}) async-start(bf16[4,32,5120]{2,0,1:T(4,128)(2,1)} %copy.67), calls=%async_computation.3 | async-start | bytes 2621440 | tf_op jit(solution)/shard_map/all_to_all | solution.py:114
  165.9 0.1 reshape.167
  166.1 33.9 %all-to-all-done.3 = bf16[4,32,5120]{2,0,1:T(4,128)(2,1)S(1)} async-done(((bf16[4,32,5120]{2,0,1:T(4,128)(2,1)}), bf16[4,32,5120]{2,0,1:T(4,128)(2,1)S(1)}, u32[]{:S(2)}, u32[]{:S(2)}) %all-to-all-start.3) | async-done | bytes 1310752 | tf_op jit(solution)/shard_map/all_to_all | solution.py:114
  200.0 0.3 reshape.173
  200.3 1.6 fusion.1
  (15 shorter events, 0.1 us)
Async XLA Ops:
  6.5 35.0 %copy-start.3 = (bf16[40,80]{1,0:T(8,128)(2,1)S(1)}, bf16[40,80]{1,0:T(8,128)(2,1)}, u32[]{:S(2)}) copy-start(bf16[40,80]{1,0:T(8,128)(2,1)} %param.11) | copy-start | bytes 19204
  6.5 83.4 %copy-start.8 = (s32[4]{0:T(128)S(1)}, s32[4]{0:T(128)}, u32[]{:S(2)}) copy-start(s32[4]{0:T(128)} %param.14) | copy-start | bytes 52
  6.5 84.1 %copy-start.6 = (s32[4]{0:T(128)S(1)}, s32[4]{0:T(128)}, u32[]{:S(2)}) copy-start(s32[4]{0:T(128)} %param.15) | copy-start | bytes 52
  6.5 91.5 %copy-start.5 = (s32[512]{0:T(512)S(1)}, s32[512]{0:T(512)}, u32[]{:S(2)}) copy-start(s32[512]{0:T(512)} %param.13) | copy-start | bytes 6148
  6.5 93.3 %copy-start.1 = (bf16[512,1280]{1,0:T(8,128)(2,1)S(1)}, bf16[512,1280]{1,0:T(8,128)(2,1)}, u32[]{:S(2)}) copy-start(bf16[512,1280]{1,0:T(8,128)(2,1)} %param.8) | copy-start | bytes 3932164
  6.6 106.3 %all-gather.3.cloned.1.call-start = ((), (), s32[]{:S(2)}) async-start(), calls=%async_computation.4 | async-start | bytes 10444800 | tf_op jit(solution)/shard_map/all_gather | solution.py:56
  7.5 105.4 %copy-start.7 = (f32[1280]{0:T(1024)S(1)}, f32[1280]{0:T(1024)}, u32[]{:S(2)}) copy-start(f32[1280]{0:T(1024)} %param.9) | copy-start | bytes 15364
  41.4 106.4 %all-gather.5.cloned.1.call-start = ((), (), s32[]{:S(2)}) async-start(), calls=%async_computation.5 | async-start | bytes 3481600 | tf_op jit(solution)/shard_map/all_gather | solution.py:86
  91.3 14.5 %all-to-all-start = ((s32[32,1,8]{2,1,0:T(1,128)}), s32[32,1,8]{2,1,0:T(1,128)S(1)}, u32[]{:S(2)}, u32[]{:S(2)}) async-start(s32[32,1,8]{2,1,0:T(1,128)} %broadcast_in_dim.96), calls=%async_computation | async-start | bytes 32768 | tf_op jit(solution)/shard_map/all_to_all | solution.py:21
  107.1 48.3 %all-to-all-start.1 = ((s32[4,32,1]{0,2,1:T(1,128)}), s32[4,32,1]{0,2,1:T(1,128)S(1)}, u32[]{:S(2)}, u32[]{:S(2)}) async-start(s32[4,32,1]{0,2,1:T(1,128)} %copy.59), calls=%async_computation.1 | async-start | bytes 32768 | tf_op jit(solution)/shard_map/all_to_all | solution.py:115
  140.2 1.6 copy-start
  144.4 3.5 %copy-start.2 = (bf16[512,1280]{1,0:T(8,128)(2,1)S(1)}, bf16[512,1280]{1,0:T(8,128)(2,1)}, u32[]{:S(2)}) copy-start(bf16[512,1280]{1,0:T(8,128)(2,1)} %param.8) | copy-start | bytes 3932164
  147.6 4.5 %copy-start.4 = (f32[1280]{0:T(1024)S(1)}, f32[1280]{0:T(1024)}, u32[]{:S(2)}) copy-start(f32[1280]{0:T(1024)} %param.12) | copy-start | bytes 15364
  155.4 44.6 %all-to-all-start.3 = ((bf16[4,32,5120]{2,0,1:T(4,128)(2,1)}), bf16[4,32,5120]{2,0,1:T(4,128)(2,1)S(1)}, u32[]{:S(2)}, u32[]{:S(2)}) async-start(bf16[4,32,5120]{2,0,1:T(4,128)(2,1)} %copy.67), calls=%async_computation.3 | async-start | bytes 2621440 | tf_op jit(solution)/shard_map/all_to_all | solution.py:114
Sparse Core Ops, SparseCore 0:
  41.6 61.6 all-gather.2
  105.4 42.3 all-gather.4
where the time goes:
time: 209 us
  blocking collectives  80.4 us (38%)
  waiting for transfers between devices  39.5 us (19%)
  local copies, waits for them, and re-layouts  27.4 us (13%)
  starting transfers between devices  23 us (11%)
  matrix products  19.4 us (9%)
  between operations  13.6 us (7%)
  other arithmetic  5.39 us (3%)
    all_gather x1, blocking collectives, body(): proj_rows = lax.all_gather(w_out, 'tensor', axis=0, tiled=True)  47.5 us
    all_to_all x1, waiting for transfers between devices, body(): lax.all_to_all(outgoing, 'tensor', split_axis=1, concat_axis=0, tiled=True)  33.9 us
    all_to_all x1, blocking collectives, copy_for_each(): lax.all_to_all(jnp.broadcast_to(x[None], (size, *x.shape)), axis, 0, 0, t...  32.9 us
    reshape x3, local copies, waits for them, and re-layouts, split_heads(): return block.reshape(tile_count, WINDOW, HEADS, head_width)  13.2 us
    all_to_all x1, starting transfers between devices, body(): lax.all_to_all(outgoing, 'tensor', split_axis=1, concat_axis=0, tiled=True)  10.5 us
    dot_general x1, matrix products, body(): jnp.dot(normed, lax.all_gather(qkv_rows, 'pipe', axis=1, tiled=True), pre...  9.5 us
    all_to_all x1, starting transfers between devices, copy_for_each(): lax.all_to_all(jnp.broadcast_to(x[None], (size, *x.shape)), axis, 0, 0, t...  6.7 us
    all_to_all x1, starting transfers between devices, body(): lax.all_to_all(outgoing_position, 'tensor', split_axis=1, concat_axis=0,...  5.71 us
  transfers between devices with their start and end apart: 5, of which 3 were waited for; matrix products, arithmetic and copies ran while one was open for 23% of the time, Pallas kernels for 0%

commit v1 on v0

--- a/solution.py
+++ b/solution.py
@@ -8,6 +8,27 @@
 WINDOW = 64
 SAMPLES = 8
 epsilon = 1e-06
+
+
+def collect(x, axis, dim):
+    size, mine, span = (lax.axis_size(axis), lax.axis_index(axis), x.shape[dim])
+    ahead = [(i, (i + 1) % size) for i in range(size)]
+    behind = [(i, (i - 1) % size) for i in range(size)]
+    whole = jnp.zeros((*x.shape[:dim], size * span, *x.shape[dim + 1 :]), x.dtype)
+    whole = lax.dynamic_update_slice_in_dim(whole, x, mine * span, axis=dim)
+    from_left = from_right = x
+    middle = size // 2
+    for step in range(1, middle + 1):
+        from_left = lax.ppermute(from_left, axis, ahead)
+        whole = lax.dynamic_update_slice_in_dim(
+            whole, from_left, (mine - step) % size * span, axis=dim
+        )
+        if step < size - middle:
+            from_right = lax.ppermute(from_right, axis, behind)
+            whole = lax.dynamic_update_slice_in_dim(
+                whole, from_right, (mine + step) % size * span, axis=dim
+            )
+    return whole
 
 
 def joined_along(blocks, dim):
@@ -81,11 +102,7 @@
     ).reshape(patch_count, feature_width)
     context = jnp.where(live_row[:, None], context, 0.0).astype(jnp.bfloat16)
     proj_rows = lax.all_gather(w_out, "tensor", axis=0, tiled=True)
-    attended = jnp.dot(
-        context,
-        lax.all_gather(proj_rows, "pipe", axis=1, tiled=True),
-        preferred_element_type=jnp.float32,
-    )
+    attended = jnp.dot(context, collect(proj_rows, "pipe", 1), preferred_element_type=jnp.float32)
     hidden = residual + attended
     merged = (
         normalize(hidden, merge_gain).astype(jnp.bfloat16).reshape(token_count, 4 * feature_width)

time: 209 us -> 332 us (1.59)
  the two profiles are of different devices: /device:TPU:4 before, /device:TPU:29 now
where the time goes in v1:
time: 332 us; the launch traced here: 329 us
  local copies, waits for them, and re-layouts  105 us (32%)
  blocking collectives  69.9 us (21%)
  starting transfers between devices  61 us (18%)
  waiting for transfers between devices  54 us (16%)
  matrix products  19.6 us (6%)
  between operations  13.9 us (4%)
  other arithmetic  5.4 us (2%)
    all_gather x1, blocking collectives, body(): proj_rows = lax.all_gather(w_out, 'tensor', axis=0, tiled=True)  38.8 us
    dynamic_update_slice x8, local copies, waits for them, and re-layouts, collect(): lax.dynamic_update_slice_in_dim(whole, from_left, (mine - step) % size *...  38 us
    ppermute x8, starting transfers between devices, collect(): from_left = lax.ppermute(from_left, axis, ahead)  37.2 us
    dynamic_update_slice x7, local copies, waits for them, and re-layouts, collect(): lax.dynamic_update_slice_in_dim(whole, from_right, (mine + step) % size *...  33.4 us
    all_to_all x1, waiting for transfers between devices, body(): lax.all_to_all(outgoing, 'tensor', split_axis=1, concat_axis=0, tiled=True)  32.9 us
    all_to_all x1, blocking collectives, copy_for_each(): lax.all_to_all(jnp.broadcast_to(x[None], (size, *x.shape)), axis, 0, 0, t...  31.1 us
    reshape x3, local copies, waits for them, and re-layouts, split_heads(): return block.reshape(tile_count, WINDOW, HEADS, head_width)  13.2 us
    ppermute x8, waiting for transfers between devices, collect(): from_left = lax.ppermute(from_left, axis, ahead)  10.6 us
  transfers between devices with their start and end apart: 19, of which 9 were waited for; matrix products, arithmetic and copies ran while one was open for 38% of the time, Pallas kernels for 0%

profile of v1, /device:TPU:29, one launch (start us, length us, event | category | flops | bytes accessed | tf_op | source)
XLA Modules:
  0.0 329.3 jit_solution(11268163681671128562)
XLA Ops:
  6.6 0.9 broadcast_in_dim.147
  7.5 31.1 %all_to_all.38 = bf16[32,40,240]{2,1,0:T(8,128)(2,1)S(1)} all-to-all(bf16[32,40,240]{2,1,0:T(8,128)(2,1)S(1)} %broadcast_in_dim.147), channel_id=1, replica_groups=mesh['pipe'=16,'tensor'=32] {'tensor'}, dimensions={0} | all-to-all | bytes 1228800 | tf_op jit(solution)/shard_map/all_to_all | solution.py:42
  38.6 1.1 copy.48
  39.7 38.8 %all_gather.7 = bf16[1280,80]{1,0:T(8,128)(2,1)S(1)} all-gather(bf16[40,80]{1,0:T(8,128)(2,1)S(1)} %copy-done.12), channel_id=1, replica_groups=mesh['pipe'=16,'tensor'=32] {'tensor'}, dimensions={0}, use_global_device_ids=true | all-gather | bytes 211200 | tf_op jit(solution)/shard_map/all_gather | solution.py:104
  78.5 13.5 %collective-permute-start = (bf16[1280,80]{1,0:T(8,128)(2,1)S(1)}, bf16[1280,80]{1,0:T(8,128)(2,1)S(1)}, u32[]{:S(2)}, u32[]{:S(2)}) collective-permute-start(bf16[1280,80]{1,0:T(8,128)(2,1)S(1)} %all_gather.7), channel_id=1, source_target_pairs={{0,32},{32,64},{64,96},{96,128},{128,160},{160,192},{192,224},{224... | collective-permute-start | bytes 614408 | tf_op jit(solution)/shard_map/ppermute | solution.py:22
  91.9 0.7 and_select_fusion.1
  92.7 0.6 broadcast_in_dim.136
  93.3 6.4 %all-to-all-start = ((s32[32,1,8]{2,1,0:T(1,128)}), s32[32,1,8]{2,1,0:T(1,128)S(1)}, u32[]{:S(2)}, u32[]{:S(2)}) async-start(s32[32,1,8]{2,1,0:T(1,128)} %broadcast_in_dim.136), calls=%async_computation | async-start | bytes 32768 | tf_op jit(solution)/shard_map/all_to_all | solution.py:42
  100.0 0.6 add_compare_fusion
  100.8 1.0 collective-permute-done
  101.8 3.7 %collective-permute-start.2 = (bf16[1280,80]{1,0:T(8,128)(2,1)S(1)}, bf16[1280,80]{1,0:T(8,128)(2,1)S(1)}, u32[]{:S(2)}, u32[]{:S(2)}) collective-permute-start(bf16[1280,80]{1,0:T(8,128)(2,1)S(1)} %collective-permute-done), channel_id=1, source_target_pairs={{0,32},{32,64},{64,96},{96,128},{128,160},{160,192},{192,224},{224... | collective-permute-start | bytes 614408 | tf_op jit(solution)/shard_map/ppermute | solution.py:22
  105.5 0.6 iota_compare_fusion.3
  106.3 3.2 collective-permute-done.2
  109.5 3.7 %collective-permute-start.4 = (bf16[1280,80]{1,0:T(8,128)(2,1)S(1)}, bf16[1280,80]{1,0:T(8,128)(2,1)S(1)}, u32[]{:S(2)}, u32[]{:S(2)}) collective-permute-start(bf16[1280,80]{1,0:T(8,128)(2,1)S(1)} %collective-permute-done.2), channel_id=1, source_target_pairs={{0,32},{32,64},{64,96},{96,128},{128,160},{160,192},{192,224},{224... | collective-permute-start | bytes 614408 | tf_op jit(solution)/shard_map/ppermute | solution.py:22
  113.4 0.5 collective-permute-done.3
  114.0 3.3 collective-permute-done.4
  117.2 3.7 %collective-permute-start.6 = (bf16[1280,80]{1,0:T(8,128)(2,1)S(1)}, bf16[1280,80]{1,0:T(8,128)(2,1)}, u32[]{:S(2)}, u32[]{:S(2)}) collective-permute-start(bf16[1280,80]{1,0:T(8,128)(2,1)S(1)} %collective-permute-done.4), channel_id=1, source_target_pairs={{0,32},{32,64},{64,96},{96,128},{128,160},{160,192},{192,224},{224... | collective-permute-start | bytes 614408 | tf_op jit(solution)/shard_map/ppermute | solution.py:22
  120.9 0.3 fusion.3
  121.3 0.5 collective-permute-done.5
  121.8 3.2 collective-permute-done.6
  124.9 3.8 %collective-permute-start.8 = (bf16[1280,80]{1,0:T(8,128)(2,1)}, bf16[1280,80]{1,0:T(8,128)(2,1)}, u32[]{:S(2)}, u32[]{:S(2)}) collective-permute-start(bf16[1280,80]{1,0:T(8,128)(2,1)} %collective-permute-done.6), channel_id=1, source_target_pairs={{0,32},{32,64},{64,96},{96,128},{128,160},{160,192},{192,224},{224... | collective-permute-start | bytes 614408 | tf_op jit(solution)/shard_map/ppermute | solution.py:22
  129.0 4.9 %dynamic_update_slice.48 = bf16[1280,1280]{1,0:T(8,128)(2,1)S(1)} dynamic-update-slice(bf16[1280,1280]{1,0:T(8,128)(2,1)S(1)} %broadcast_in_dim.151, bf16[1280,80]{1,0:T(8,128)(2,1)} %copy-done.4, s32[]{:T(128)} %constant.130.clone.1, s32[]{:T(128)S(6)} %select_n.184) | dynamic-update-slice | bytes 409604 | tf_op jit(solution)/shard_map/dynamic_update_slice | solution.py:18
  134.1 2.9 collective-permute-start.10
  137.2 4.7 %collective-permute-done.9 = bf16[1280,80]{1,0:T(8,128)(2,1)S(1)} collective-permute-done((bf16[1280,80]{1,0:T(8,128)(2,1)}, bf16[1280,80]{1,0:T(8,128)(2,1)S(1)}, u32[]{:S(2)}, u32[]{:S(2)}) %collective-permute-start.9) | collective-permute-done | bytes 204832 | tf_op jit(solution)/shard_map/ppermute | solution.py:27
  142.0 0.7 copy-done.10
  142.7 3.0 collective-permute-start.12
  145.9 4.6 %collective-permute-done.11 = bf16[1280,80]{1,0:T(8,128)(2,1)} collective-permute-done((bf16[1280,80]{1,0:T(8,128)(2,1)S(1)}, bf16[1280,80]{1,0:T(8,128)(2,1)}, u32[]{:S(2)}, u32[]{:S(2)}) %collective-permute-start.11) | collective-permute-done | bytes 204832 | tf_op jit(solution)/shard_map/ppermute | solution.py:27
  150.5 3.0 collective-permute-start.14
  153.6 0.7 copy.47
  154.3 8.1 %all-to-all-start.1 = ((s32[4,32,1]{0,2,1:T(1,128)}), s32[4,32,1]{0,2,1:T(1,128)S(1)}, u32[]{:S(2)}, u32[]{:S(2)}) async-start(s32[4,32,1]{0,2,1:T(1,128)} %copy.47), calls=%async_computation.1 | async-start | bytes 32768 | tf_op jit(solution)/shard_map/all_to_all | solution.py:132
  162.4 4.9 %dynamic_update_slice.49 = bf16[1280,1280]{1,0:T(8,128)(2,1)S(1)} dynamic-update-slice(bf16[1280,1280]{1,0:T(8,128)(2,1)S(1)} %dynamic_update_slice.48, bf16[1280,80]{1,0:T(8,128)(2,1)} %copy-done.5, s32[]{:T(128)} %constant.130.clone.1, s32[]{:T(128)S(6)} %select_n.186) | dynamic-update-slice | bytes 409604 | tf_op jit(solution)/shard_map/dynamic_update_slice | solution.py:23
  167.3 4.1 %dynamic_update_slice.50 = bf16[1280,1280]{1,0:T(8,128)(2,1)S(1)} dynamic-update-slice(bf16[1280,1280]{1,0:T(8,128)(2,1)S(1)} %dynamic_update_slice.49, bf16[1280,80]{1,0:T(8,128)(2,1)} %copy-done.6, s32[]{:T(128)} %constant.130.clone.1, s32[]{:T(128)S(6)} %select_n.188) | dynamic-update-slice | bytes 409604 | tf_op jit(solution)/shard_map/dynamic_update_slice | solution.py:28
  171.3 4.9 %dynamic_update_slice.51 = bf16[1280,1280]{1,0:T(8,128)(2,1)S(1)} dynamic-update-slice(bf16[1280,1280]{1,0:T(8,128)(2,1)S(1)} %dynamic_update_slice.50, bf16[1280,80]{1,0:T(8,128)(2,1)} %copy-done.7, s32[]{:T(128)} %constant.130.clone.1, s32[]{:T(128)S(6)} %select_n.190) | dynamic-update-slice | bytes 409604 | tf_op jit(solution)/shard_map/dynamic_update_slice | solution.py:23
  176.2 4.9 %dynamic_update_slice.52 = bf16[1280,1280]{1,0:T(8,128)(2,1)S(1)} dynamic-update-slice(bf16[1280,1280]{1,0:T(8,128)(2,1)S(1)} %dynamic_update_slice.51, bf16[1280,80]{1,0:T(8,128)(2,1)} %copy-done.8, s32[]{:T(128)} %constant.130.clone.1, s32[]{:T(128)S(6)} %select_n.192) | dynamic-update-slice | bytes 409604 | tf_op jit(solution)/shard_map/dynamic_update_slice | solution.py:28
  181.1 4.9 %dynamic_update_slice.53 = bf16[1280,1280]{1,0:T(8,128)(2,1)S(1)} dynamic-update-slice(bf16[1280,1280]{1,0:T(8,128)(2,1)S(1)} %dynamic_update_slice.52, bf16[1280,80]{1,0:T(8,128)(2,1)} %copy-done.9, s32[]{:T(128)} %constant.130.clone.1, s32[]{:T(128)S(6)} %select_n.194) | dynamic-update-slice | bytes 409604 | tf_op jit(solution)/shard_map/dynamic_update_slice | solution.py:23
  186.0 4.9 %dynamic_update_slice.54 = bf16[1280,1280]{1,0:T(8,128)(2,1)S(1)} dynamic-update-slice(bf16[1280,1280]{1,0:T(8,128)(2,1)S(1)} %dynamic_update_slice.53, bf16[1280,80]{1,0:T(8,128)(2,1)} %collective-permute-done.5, s32[]{:T(128)} %constant.130.clone.1, s32[]{:T(128)S(6)} %select_n.196) | dynamic-update-slice | bytes 409604 | tf_op jit(solution)/shard_map/dynamic_update_slice | solution.py:28
  190.9 4.9 %dynamic_update_slice.55 = bf16[1280,1280]{1,0:T(8,128)(2,1)S(1)} dynamic-update-slice(bf16[1280,1280]{1,0:T(8,128)(2,1)S(1)} %dynamic_update_slice.54, bf16[1280,80]{1,0:T(8,128)(2,1)} %collective-permute-done.6, s32[]{:T(128)} %constant.130.clone.1, s32[]{:T(128)S(6)} %select_n.198) | dynamic-update-slice | bytes 409604 | tf_op jit(solution)/shard_map/dynamic_update_slice | solution.py:23
  195.8 4.9 %dynamic_update_slice.56 = bf16[1280,1280]{1,0:T(8,128)(2,1)S(1)} dynamic-update-slice(bf16[1280,1280]{1,0:T(8,128)(2,1)S(1)} %dynamic_update_slice.55, bf16[1280,80]{1,0:T(8,128)(2,1)} %collective-permute-done.7, s32[]{:T(128)} %constant.130.clone.1, s32[]{:T(128)S(6)} %select_n.200) | dynamic-update-slice | bytes 409604 | tf_op jit(solution)/shard_map/dynamic_update_slice | solution.py:28
  200.7 4.9 %dynamic_update_slice.57 = bf16[1280,1280]{1,0:T(8,128)(2,1)S(1)} dynamic-update-slice(bf16[1280,1280]{1,0:T(8,128)(2,1)S(1)} %dynamic_update_slice.56, bf16[1280,80]{1,0:T(8,128)(2,1)} %collective-permute-done.8, s32[]{:T(128)} %constant.130.clone.1, s32[]{:T(128)S(6)} %select_n.202) | dynamic-update-slice | bytes 409604 | tf_op jit(solution)/shard_map/dynamic_update_slice | solution.py:23
  205.6 4.9 %dynamic_update_slice.58 = bf16[1280,1280]{1,0:T(8,128)(2,1)S(1)} dynamic-update-slice(bf16[1280,1280]{1,0:T(8,128)(2,1)S(1)} %dynamic_update_slice.57, bf16[1280,80]{1,0:T(8,128)(2,1)} %copy-done.10, s32[]{:T(128)} %constant.130.clone.1, s32[]{:T(128)S(6)} %select_n.204) | dynamic-update-slice | bytes 409604 | tf_op jit(solution)/shard_map/dynamic_update_slice | solution.py:28
  210.5 4.9 %dynamic_update_slice.59 = bf16[1280,1280]{1,0:T(8,128)(2,1)S(1)} dynamic-update-slice(bf16[1280,1280]{1,0:T(8,128)(2,1)S(1)} %dynamic_update_slice.58, bf16[1280,80]{1,0:T(8,128)(2,1)} %copy-done.11, s32[]{:T(128)} %constant.130.clone.1, s32[]{:T(128)S(6)} %select_n.206) | dynamic-update-slice | bytes 409604 | tf_op jit(solution)/shard_map/dynamic_update_slice | solution.py:23
  215.4 4.9 %dynamic_update_slice.60 = bf16[1280,1280]{1,0:T(8,128)(2,1)S(1)} dynamic-update-slice(bf16[1280,1280]{1,0:T(8,128)(2,1)S(1)} %dynamic_update_slice.59, bf16[1280,80]{1,0:T(8,128)(2,1)} %collective-permute-done.11, s32[]{:T(128)} %constant.130.clone.1, s32[]{:T(128)S(6)} %select_n.208) | dynamic-update-slice | bytes 409604 | tf_op jit(solution)/shard_map/dynamic_update_slice | solution.py:28
  220.3 4.1 %dynamic_update_slice.61 = bf16[1280,1280]{1,0:T(8,128)(2,1)S(1)} dynamic-update-slice(bf16[1280,1280]{1,0:T(8,128)(2,1)S(1)} %dynamic_update_slice.60, bf16[1280,80]{1,0:T(8,128)(2,1)} %collective-permute-done.12, s32[]{:T(128)} %constant.130.clone.1, s32[]{:T(128)S(6)} %select_n.210) | dynamic-update-slice | bytes 409604 | tf_op jit(solution)/shard_map/dynamic_update_slice | solution.py:23
  224.4 4.9 %dynamic_update_slice.62 = bf16[1280,1280]{1,0:T(8,128)(2,1)S(1)} dynamic-update-slice(bf16[1280,1280]{1,0:T(8,128)(2,1)S(1)} %dynamic_update_slice.61, bf16[1280,80]{1,0:T(8,128)(2,1)} %collective-permute-done.13, s32[]{:T(128)} %constant.130.clone.1, s32[]{:T(128)S(6)} %select_n.212) | dynamic-update-slice | bytes 409604 | tf_op jit(solution)/shard_map/dynamic_update_slice | solution.py:28
  229.3 4.6 %dynamic_update_slice.63 = bf16[1280,1280]{1,0:T(8,128)(2,1)S(1)} dynamic-update-slice(bf16[1280,1280]{1,0:T(8,128)(2,1)S(1)} %dynamic_update_slice.62, bf16[1280,80]{1,0:T(8,128)(2,1)} %collective-permute-done.14, s32[]{:T(128)} %constant.130.clone.1, s32[]{:T(128)S(6)} %select_n.214) | dynamic-update-slice | bytes 409604 | tf_op jit(solution)/shard_map/dynamic_update_slice | solution.py:23
  234.0 1.7 copy-done
  235.7 9.7 %convolution_convert_fusion.1 = bf16[512,3840]{1,0:T(8,128)(2,1)S(1)} fusion(bf16[1280,3840]{0,1:T(8,128)(2,1)} %all-gather.2.cloned.1.call-done, bf16[512,1280]{1,0:T(8,128)(2,1)} %param.8, f32[1280]{0:T(1024)S(1)} %copy-done.16, f32[512]{0:T(512)S(1)} %add_rsqrt_fusion.1), kind=kOutput, calls=%fused_computation.2 | convolution fusion | flops 5037752320 | bytes 15080448 | tf_op jit(solution)/shard_map/dot_general | solution.py:75
  245.4 1.8 fusion.26
  247.1 4.1 %reshape.170 = bf16[8,64,16,80]{3,2,1,0:T(8,128)(2,1)S(1)} reshape(bf16[512,1280]{1,0:T(8,128)(2,1)} %get-tuple-element.7) | data formatting | bytes 2621440 | tf_op jit(solution)/shard_map/reshape | solution.py:84
  251.2 5.0 %reshape.171 = bf16[8,64,16,80]{3,2,1,0:T(8,128)(2,1)} reshape(bf16[512,1280]{1,0:T(8,128)(2,1)} %get-tuple-element.6) | data formatting | bytes 2621440 | tf_op jit(solution)/shard_map/reshape | solution.py:84
  256.3 4.1 %reshape.169 = bf16[8,64,16,80]{3,2,1,0:T(8,128)(2,1)} reshape(bf16[512,1280]{1,0:T(8,128)(2,1)S(1)} %get-tuple-element.5) | data formatting | bytes 2621440 | tf_op jit(solution)/shard_map/reshape | solution.py:84
  260.3 2.8 fusion.7
  263.2 1.5 fusion.27
  264.8 1.2 convolution_bitcast_fusion
  265.9 1.4 copy.53
  267.3 3.3 reshape.172
  270.6 4.4 %multiply_reduce_fusion = (f32[512]{0:T(512)S(1)}, f32[512,1280]{1,0:T(8,128)S(1)}) fusion(bf16[1280,1280]{1,0:T(8,128)(2,1)} %copy-done, bf16[512,1280]{1,0:T(8,128)(2,1)} %reshape.172, pred[512]{0:T(512)(128)(4,1)S(1)} %iota_compare_fusion.3, bf16[512,1280]{1,0:T(8,128)(2,1)S(1)} %copy-done.3), kind=kOutput, calls=%fused_computation.15 | convolution fusion | flops 1680997888 | bytes 8522240 | tf_op jit(solution)/shard_map/dot_general | solution.py:105
  275.0 0.3 multiply_convert_fusion
  275.3 0.8 reshape_reshape.3
  276.1 2.1 copy.54
  278.2 9.2 %all-to-all-start.3 = ((bf16[4,32,5120]{2,0,1:T(4,128)(2,1)}), bf16[4,32,5120]{2,0,1:T(4,128)(2,1)S(1)}, u32[]{:S(2)}, u32[]{:S(2)}) async-start(bf16[4,32,5120]{2,0,1:T(4,128)(2,1)} %copy.54), calls=%async_computation.3 | async-start | bytes 2621440 | tf_op jit(solution)/shard_map/all_to_all | solution.py:131
  287.6 32.9 %all-to-all-done.3 = bf16[4,32,5120]{2,0,1:T(4,128)(2,1)S(1)} async-done(((bf16[4,32,5120]{2,0,1:T(4,128)(2,1)}), bf16[4,32,5120]{2,0,1:T(4,128)(2,1)S(1)}, u32[]{:S(2)}, u32[]{:S(2)}) %all-to-all-start.3) | async-done | bytes 1310752 | tf_op jit(solution)/shard_map/all_to_all | solution.py:131
  320.5 0.3 reshape.173
  320.9 1.6 fusion.1
  (76 shorter events, 2.1 us)
Async XLA Ops:
  6.5 33.1 %copy-start.12 = (bf16[40,80]{1,0:T(8,128)(2,1)S(1)}, bf16[40,80]{1,0:T(8,128)(2,1)}, u32[]{:S(2)}) copy-start(bf16[40,80]{1,0:T(8,128)(2,1)} %param.11) | copy-start | bytes 19204
  6.5 85.4 %copy-start.17 = (s32[4]{0:T(128)S(1)}, s32[4]{0:T(128)}, u32[]{:S(2)}) copy-start(s32[4]{0:T(128)} %param.14) | copy-start | bytes 52
  6.5 86.1 %copy-start.15 = (s32[4]{0:T(128)S(1)}, s32[4]{0:T(128)}, u32[]{:S(2)}) copy-start(s32[4]{0:T(128)} %param.15) | copy-start | bytes 52
  6.5 93.2 %copy-start.14 = (s32[512]{0:T(512)S(1)}, s32[512]{0:T(512)}, u32[]{:S(2)}) copy-start(s32[512]{0:T(512)} %param.13) | copy-start | bytes 6148
  6.5 114.4 %copy-start.2 = (bf16[512,1280]{1,0:T(8,128)(2,1)S(1)}, bf16[512,1280]{1,0:T(8,128)(2,1)}, u32[]{:S(2)}) copy-start(bf16[512,1280]{1,0:T(8,128)(2,1)} %param.8) | copy-start | bytes 3932164
  6.6 227.4 %all-gather.2.cloned.1.call-start = ((), (), s32[]{:S(2)}) async-start(), calls=%async_computation.4 | async-start | bytes 10444800 | tf_op jit(solution)/shard_map/all_gather | solution.py:77
  78.4 50.3 %copy-start.4 = (bf16[1280,80]{1,0:T(8,128)(2,1)}, bf16[1280,80]{1,0:T(8,128)(2,1)S(1)}, u32[]{:S(2)}) copy-start(bf16[1280,80]{1,0:T(8,128)(2,1)S(1)} %all_gather.7) | copy-start | bytes 614404
  78.5 23.3 %collective-permute-start = (bf16[1280,80]{1,0:T(8,128)(2,1)S(1)}, bf16[1280,80]{1,0:T(8,128)(2,1)S(1)}, u32[]{:S(2)}, u32[]{:S(2)}) collective-permute-start(bf16[1280,80]{1,0:T(8,128)(2,1)S(1)} %all_gather.7), channel_id=1, source_target_pairs={{0,32},{32,64},{64,96},{96,128},{128,160},{160,192},{192,224},{224... | collective-permute-start | bytes 614408 | tf_op jit(solution)/shard_map/ppermute | solution.py:22
  91.9 14.3 %collective-permute-start.1 = (bf16[1280,80]{1,0:T(8,128)(2,1)S(1)}, bf16[1280,80]{1,0:T(8,128)(2,1)S(1)}, u32[]{:S(2)}, u32[]{:S(2)}) collective-permute-start(bf16[1280,80]{1,0:T(8,128)(2,1)S(1)} %all_gather.7), channel_id=1, source_target_pairs={{0,480},{32,0},{64,32},{96,64},{128,96},{160,128},{192,160},{224,1... | collective-permute-start | bytes 614408 | tf_op jit(solution)/shard_map/ppermute | solution.py:27
  93.3 40.6 %all-to-all-start = ((s32[32,1,8]{2,1,0:T(1,128)}), s32[32,1,8]{2,1,0:T(1,128)S(1)}, u32[]{:S(2)}, u32[]{:S(2)}) async-start(s32[32,1,8]{2,1,0:T(1,128)} %broadcast_in_dim.136), calls=%async_computation | async-start | bytes 32768 | tf_op jit(solution)/shard_map/all_to_all | solution.py:42
  101.8 26.9 %copy-start.5 = (bf16[1280,80]{1,0:T(8,128)(2,1)}, bf16[1280,80]{1,0:T(8,128)(2,1)S(1)}, u32[]{:S(2)}) copy-start(bf16[1280,80]{1,0:T(8,128)(2,1)S(1)} %collective-permute-done) | copy-start | bytes 614404
  101.8 7.7 %collective-permute-start.2 = (bf16[1280,80]{1,0:T(8,128)(2,1)S(1)}, bf16[1280,80]{1,0:T(8,128)(2,1)S(1)}, u32[]{:S(2)}, u32[]{:S(2)}) collective-permute-start(bf16[1280,80]{1,0:T(8,128)(2,1)S(1)} %collective-permute-done), channel_id=1, source_target_pairs={{0,32},{32,64},{64,96},{96,128},{128,160},{160,192},{192,224},{224... | collective-permute-start | bytes 614408 | tf_op jit(solution)/shard_map/ppermute | solution.py:22
  106.2 22.5 %copy-start.6 = (bf16[1280,80]{1,0:T(8,128)(2,1)}, bf16[1280,80]{1,0:T(8,128)(2,1)S(1)}, u32[]{:S(2)}) copy-start(bf16[1280,80]{1,0:T(8,128)(2,1)S(1)} %collective-permute-done.1) | copy-start | bytes 614404
  106.2 7.7 %collective-permute-start.3 = (bf16[1280,80]{1,0:T(8,128)(2,1)S(1)}, bf16[1280,80]{1,0:T(8,128)(2,1)S(1)}, u32[]{:S(2)}, u32[]{:S(2)}) collective-permute-start(bf16[1280,80]{1,0:T(8,128)(2,1)S(1)} %collective-permute-done.1), channel_id=1, source_target_pairs={{0,480},{32,0},{64,32},{96,64},{128,96},{160,128},{192,160},{224,1... | collective-permute-start | bytes 614408 | tf_op jit(solution)/shard_map/ppermute | solution.py:27
  109.5 4.5 %copy-start.7 = (bf16[1280,80]{1,0:T(8,128)(2,1)}, bf16[1280,80]{1,0:T(8,128)(2,1)S(1)}, u32[]{:S(2)}) copy-start(bf16[1280,80]{1,0:T(8,128)(2,1)S(1)} %collective-permute-done.2) | copy-start | bytes 614404
  109.5 7.7 %collective-permute-start.4 = (bf16[1280,80]{1,0:T(8,128)(2,1)S(1)}, bf16[1280,80]{1,0:T(8,128)(2,1)S(1)}, u32[]{:S(2)}, u32[]{:S(2)}) collective-permute-start(bf16[1280,80]{1,0:T(8,128)(2,1)S(1)} %collective-permute-done.2), channel_id=1, source_target_pairs={{0,32},{32,64},{64,96},{96,128},{128,160},{160,192},{192,224},{224... | collective-permute-start | bytes 614408 | tf_op jit(solution)/shard_map/ppermute | solution.py:22
  114.0 14.8 %copy-start.8 = (bf16[1280,80]{1,0:T(8,128)(2,1)}, bf16[1280,80]{1,0:T(8,128)(2,1)S(1)}, u32[]{:S(2)}) copy-start(bf16[1280,80]{1,0:T(8,128)(2,1)S(1)} %collective-permute-done.3) | copy-start | bytes 614404
  114.0 7.8 %collective-permute-start.5 = (bf16[1280,80]{1,0:T(8,128)(2,1)S(1)}, bf16[1280,80]{1,0:T(8,128)(2,1)}, u32[]{:S(2)}, u32[]{:S(2)}) collective-permute-start(bf16[1280,80]{1,0:T(8,128)(2,1)S(1)} %collective-permute-done.3), channel_id=1, source_target_pairs={{0,480},{32,0},{64,32},{96,64},{128,96},{160,128},{192,160},{224,1... | collective-permute-start | bytes 614408 | tf_op jit(solution)/shard_map/ppermute | solution.py:27
  117.2 11.5 %copy-start.9 = (bf16[1280,80]{1,0:T(8,128)(2,1)}, bf16[1280,80]{1,0:T(8,128)(2,1)S(1)}, u32[]{:S(2)}) copy-start(bf16[1280,80]{1,0:T(8,128)(2,1)S(1)} %collective-permute-done.4) | copy-start | bytes 614404
  117.2 7.7 %collective-permute-start.6 = (bf16[1280,80]{1,0:T(8,128)(2,1)S(1)}, bf16[1280,80]{1,0:T(8,128)(2,1)}, u32[]{:S(2)}, u32[]{:S(2)}) collective-permute-start(bf16[1280,80]{1,0:T(8,128)(2,1)S(1)} %collective-permute-done.4), channel_id=1, source_target_pairs={{0,32},{32,64},{64,96},{96,128},{128,160},{160,192},{192,224},{224... | collective-permute-start | bytes 614408 | tf_op jit(solution)/shard_map/ppermute | solution.py:22
  121.8 12.3 %collective-permute-start.7 = (bf16[1280,80]{1,0:T(8,128)(2,1)}, bf16[1280,80]{1,0:T(8,128)(2,1)}, u32[]{:S(2)}, u32[]{:S(2)}) collective-permute-start(bf16[1280,80]{1,0:T(8,128)(2,1)} %collective-permute-done.5), channel_id=1, source_target_pairs={{0,480},{32,0},{64,32},{96,64},{128,96},{160,128},{192,160},{224,1... | collective-permute-start | bytes 614408 | tf_op jit(solution)/shard_map/ppermute | solution.py:27
  124.9 9.1 %collective-permute-start.8 = (bf16[1280,80]{1,0:T(8,128)(2,1)}, bf16[1280,80]{1,0:T(8,128)(2,1)}, u32[]{:S(2)}, u32[]{:S(2)}) collective-permute-start(bf16[1280,80]{1,0:T(8,128)(2,1)} %collective-permute-done.6), channel_id=1, source_target_pairs={{0,32},{32,64},{64,96},{96,128},{128,160},{160,192},{192,224},{224... | collective-permute-start | bytes 614408 | tf_op jit(solution)/shard_map/ppermute | solution.py:22
  134.0 7.9 %collective-permute-start.9 = (bf16[1280,80]{1,0:T(8,128)(2,1)}, bf16[1280,80]{1,0:T(8,128)(2,1)S(1)}, u32[]{:S(2)}, u32[]{:S(2)}) collective-permute-start(bf16[1280,80]{1,0:T(8,128)(2,1)} %collective-permute-done.7), channel_id=1, source_target_pairs={{0,480},{32,0},{64,32},{96,64},{128,96},{160,128},{192,160},{224,1... | collective-permute-start | bytes 614408 | tf_op jit(solution)/shard_map/ppermute | solution.py:27
  134.1 8.6 %collective-permute-start.10 = (bf16[1280,80]{1,0:T(8,128)(2,1)}, bf16[1280,80]{1,0:T(8,128)(2,1)S(1)}, u32[]{:S(2)}, u32[]{:S(2)}) collective-permute-start(bf16[1280,80]{1,0:T(8,128)(2,1)} %collective-permute-done.8), channel_id=1, source_target_pairs={{0,32},{32,64},{64,96},{96,128},{128,160},{160,192},{192,224},{224... | collective-permute-start | bytes 614408 | tf_op jit(solution)/shard_map/ppermute | solution.py:22
  142.0 0.7 copy-start.10
  142.7 7.8 %collective-permute-start.11 = (bf16[1280,80]{1,0:T(8,128)(2,1)S(1)}, bf16[1280,80]{1,0:T(8,128)(2,1)}, u32[]{:S(2)}, u32[]{:S(2)}) collective-permute-start(bf16[1280,80]{1,0:T(8,128)(2,1)S(1)} %collective-permute-done.9), channel_id=1, source_target_pairs={{0,480},{32,0},{64,32},{96,64},{128,96},{160,128},{192,160},{224,1... | collective-permute-start | bytes 614408 | tf_op jit(solution)/shard_map/ppermute | solution.py:27
  142.7 7.8 %copy-start.11 = (bf16[1280,80]{1,0:T(8,128)(2,1)}, bf16[1280,80]{1,0:T(8,128)(2,1)S(1)}, u32[]{:S(2)}) copy-start(bf16[1280,80]{1,0:T(8,128)(2,1)S(1)} %collective-permute-done.10) | copy-start | bytes 614404
  142.7 7.8 %collective-permute-start.12 = (bf16[1280,80]{1,0:T(8,128)(2,1)S(1)}, bf16[1280,80]{1,0:T(8,128)(2,1)}, u32[]{:S(2)}, u32[]{:S(2)}) collective-permute-start(bf16[1280,80]{1,0:T(8,128)(2,1)S(1)} %collective-permute-done.10), channel_id=1, source_target_pairs={{0,32},{32,64},{64,96},{96,128},{128,160},{160,192},{192,224},{224... | collective-permute-start | bytes 614408 | tf_op jit(solution)/shard_map/ppermute | solution.py:22
  150.5 73.8 %collective-permute-start.13 = (bf16[1280,80]{1,0:T(8,128)(2,1)}, bf16[1280,80]{1,0:T(8,128)(2,1)}, u32[]{:S(2)}, u32[]{:S(2)}) collective-permute-start(bf16[1280,80]{1,0:T(8,128)(2,1)} %collective-permute-done.11), channel_id=1, source_target_pairs={{0,480},{32,0},{64,32},{96,64},{128,96},{160,128},{192,160},{224,1... | collective-permute-start | bytes 614408 | tf_op jit(solution)/shard_map/ppermute | solution.py:27
  150.5 78.7 %collective-permute-start.14 = (bf16[1280,80]{1,0:T(8,128)(2,1)}, bf16[1280,80]{1,0:T(8,128)(2,1)}, u32[]{:S(2)}, u32[]{:S(2)}) collective-permute-start(bf16[1280,80]{1,0:T(8,128)(2,1)} %collective-permute-done.12), channel_id=1, source_target_pairs={{0,32},{32,64},{64,96},{96,128},{128,160},{160,192},{192,224},{224... | collective-permute-start | bytes 614408 | tf_op jit(solution)/shard_map/ppermute | solution.py:22
  154.3 124.0 %all-to-all-start.1 = ((s32[4,32,1]{0,2,1:T(1,128)}), s32[4,32,1]{0,2,1:T(1,128)S(1)}, u32[]{:S(2)}, u32[]{:S(2)}) async-start(s32[4,32,1]{0,2,1:T(1,128)} %copy.47), calls=%async_computation.1 | async-start | bytes 32768 | tf_op jit(solution)/shard_map/all_to_all | solution.py:132
  195.8 39.8 %copy-start.16 = (f32[1280]{0:T(1024)S(1)}, f32[1280]{0:T(1024)}, u32[]{:S(2)}) copy-start(f32[1280]{0:T(1024)} %param.9) | copy-start | bytes 15364
  233.9 1.7 copy-start
  263.2 1.6 copy-start.1
  267.3 3.3 copy-start.3
  270.6 4.4 %copy-start.13 = (f32[1280]{0:T(1024)S(1)}, f32[1280]{0:T(1024)}, u32[]{:S(2)}) copy-start(f32[1280]{0:T(1024)} %param.12) | copy-start | bytes 15364
  278.2 42.3 %all-to-all-start.3 = ((bf16[4,32,5120]{2,0,1:T(4,128)(2,1)}), bf16[4,32,5120]{2,0,1:T(4,128)(2,1)S(1)}, u32[]{:S(2)}, u32[]{:S(2)}) async-start(bf16[4,32,5120]{2,0,1:T(4,128)(2,1)} %copy.54), calls=%async_computation.3 | async-start | bytes 2621440 | tf_op jit(solution)/shard_map/all_to_all | solution.py:131
Sparse Core Ops, SparseCore 0:
  39.8 65.9 all-gather.1
